TPU v7x, 32 devices: a whole 2x2x4 slice. The times are simulated.
32 devices in a mesh: row: 4 (over z), col: 8 (over y, x, core).
Axes of the slice: x: 2, y: 2, z: 4, core: 2. Of those that a mesh axis runs over, the one named last changes fastest.
Arguments:
- operator: bfloat16 [32768, 32768], P('row', 'col'), may hold values from -6 to 6
- right_test: bfloat16 [32768, 256], P('col'), may hold values from -0.03125 to 0.03125
- left_test: bfloat16 [32768, 384], P('row'), may hold values from -0.03125 to 0.03125
Outputs:
- left_factor: bfloat16 [32768, 256], P(('row', 'col'))
- right_factor: bfloat16 [32768, 256], P('col')
All inputs are finite; a program needn't handle non-finite values.
Results may differ from a plain program's by a relative error of at most 0.0015.
Values may be sent and summed in bfloat16 or wider, within the bound.
A program may use at most 192 MiB of HBM per device.

v0:
```python
import jax
import jax.numpy as jnp
from jax import lax
from jax.sharding import PartitionSpec as P


def body(operator, right_test, left_test):
    width_right = right_test.shape[1]
    block_left = jnp.dot(operator, right_test, preferred_element_type=jnp.float32)
    block_core = lax.dot_general(
        left_test.astype(jnp.float32),
        block_left,
        (((0,), (0,)), ((), ())),
        precision=lax.Precision.HIGHEST,
    )
    core_matrix = lax.psum(block_core, ("row", "col"))
    left_share = lax.psum_scatter(block_left, "col", scatter_dimension=0, tiled=True)
    right_whole = lax.psum(
        lax.dot_general(
            operator, left_test, (((0,), (0,)), ((), ())), preferred_element_type=jnp.float32
        ),
        "row",
    )
    gram_plain = jnp.dot(core_matrix.T, core_matrix, precision=lax.Precision.HIGHEST)
    shift_size = 0.001 * jnp.trace(gram_plain) / width_right
    gram_matrix = gram_plain + shift_size * jnp.eye(width_right, dtype=jnp.float32)
    lower_factor = jnp.linalg.cholesky(gram_matrix)
    solve_map = jax.scipy.linalg.cho_solve((lower_factor, True), core_matrix.T)
    right_factor = jnp.dot(right_whole, solve_map.T, precision=lax.Precision.HIGHEST).astype(
        jnp.bfloat16
    )
    return (left_share.astype(jnp.bfloat16), right_factor)


def solution(mesh):
    placed = (P("row", "col"), P("col", None), P("row", None))
    return jax.shard_map(
        body,
        mesh=mesh,
        in_specs=placed,
        out_specs=(P(("row", "col"), None), P("col", None)),
        check_vma=False,
    )
```

profile of v0, /device:TPU:0, one launch (start us, length us, event | category | flops | bytes accessed | tf_op | source)
XLA Modules:
  0.0 432.1 jit_solution(15498314063320386907)
XLA Ops:
  8.1 1.5 copy-done
  9.6 28.9 %fusion.17 = f32[8192,256]{1,0:T(8,128)} fusion(bf16[8192,4096]{1,0:T(8,128)(2,1)} %param.3, bf16[4096,256]{1,0:T(8,128)(2,1)S(1)} %copy-done), kind=kOutput, calls=%fused_computation.42 | convolution fusion | flops 17179869184 | bytes 77594624 | tf_op jit(solution)/shard_map/dot_general | solution.py:9
  38.5 10.9 %convolution_bitcast_fusion = f32[384,256]{0,1:T(8,128)} fusion(f32[8192,256]{1,0:T(8,128)} %fusion.17, bf16[8192,384]{1,0:T(8,128)(2,1)} %param.5), kind=kOutput, calls=%fused_computation.3 | convolution fusion | flops 9663676416 | bytes 15073280 | tf_op jit(solution)/shard_map/dot_general | solution.py:10
  49.4 42.3 %fusion.18 = f32[4096,384]{1,0:T(8,128)} fusion(bf16[8192,4096]{1,0:T(8,128)(2,1)} %param.3, bf16[8192,384]{1,0:T(8,128)(2,1)} %param.5), kind=kOutput, calls=%fused_computation.43 | convolution fusion | flops 25769803776 | bytes 79691776 | tf_op jit(solution)/shard_map/dot_general | solution.py:19
  91.9 0.3 reduce-scatter.2.cloned.1.call-update
  92.3 96.1 %all-reduce.6.cloned.1.call-done = f32[384,256]{0,1:T(8,128)} async-done(((f32[384,256]{0,1:T(8,128)}), f32[384,256]{0,1:T(8,128)}) %all-reduce.6.cloned.1.call-update) | async-done | bytes 393232 | tf_op jit(solution)/shard_map/psum | solution.py:16
  188.5 2.3 select_reduce_fusion
  191.7 11.7 %cholesky.49 = f32[128,128]{1,0:T(8,128)S(1)} custom-call(f32[128,128]{1,0:T(8,128)S(1)} %cholesky.115), custom_call_target="Cholesky" | custom-call | tf_op jit(solution)/shard_map/jit(cholesky)/cholesky | solution.py:27
  203.4 9.8 %custom-call.18 = f32[1,128,128]{1,2,0:T(8,128)S(1)} custom-call(f32[1,128,128]{2,1,0:T(8,128)S(1)} %get-tuple-element.23), custom_call_target="InvertDiagBlocksLowerTriangular" | custom-call | tf_op jit(solution)/shard_map/jit(cholesky)/cholesky | solution.py:27
  213.7 11.7 %cholesky.103 = f32[128,128]{1,0:T(8,128)S(1)} custom-call(f32[128,128]{1,0:T(8,128)S(1)} %convolution_subtract_fusion.2), custom_call_target="Cholesky" | custom-call | tf_op jit(solution)/shard_map/jit(cholesky)/cholesky | solution.py:27
  225.5 0.6 compare_reduce_fusion
  227.4 4.0 while.1
  227.6 0.6 fusion.36
  228.2 1.3 bitcast_dynamic-update-slice_fusion.2
  229.5 0.6 fusion.36
  230.1 1.3 bitcast_dynamic-update-slice_fusion.2
  231.4 19.7 %custom-call.19 = f32[2,128,128]{1,2,0:T(8,128)S(1)} custom-call(f32[2,128,128]{2,1,0:T(8,128)S(1)} %get-tuple-element.9), custom_call_target="InvertDiagBlocksLowerTriangular" | custom-call | tf_op jit(solution)/shard_map/jit(_cho_solve)/triangular_solve | solution.py:28
  251.1 1.3 fusion.5
  252.4 1.2 convolution_subtract_fusion.1
  253.7 0.4 fusion.12
  254.4 0.4 convolution_subtract_fusion
  255.1 157.7 %all-reduce.4.cloned.1.call-done = f32[4096,384]{1,0:T(8,128)} async-done(((f32[4096,384]{1,0:T(8,128)}), f32[4096,384]{1,0:T(8,128)}) %all-reduce.4.cloned.1.call-update) | async-done | bytes 6291472 | tf_op jit(solution)/shard_map/psum | solution.py:18
  412.8 9.8 %convolution_convert_fusion = bf16[4096,256]{1,0:T(8,128)(2,1)} fusion(f32[4096,384]{1,0:T(8,128)} %all-reduce.4.cloned.1.call-done, f32[128,384]{1,0:T(8,128)S(1)} %fusion.11, f32[128,384]{1,0:T(8,128)S(1)} %fusion.10), kind=kOutput, calls=%fused_computation.2 | convolution fusion | flops 4832985088 | bytes 8781824 | tf_op jit(solution)/shard_map/dot_general | solution.py:29
  422.6 2.1 convert_element_type.8
  (23 shorter events, 1.8 us)
Async XLA Ops:
  8.0 1.6 copy-start
  8.0 180.4 %all-reduce.6.cloned.1.call-start = ((), (), s32[]{:S(2)}) async-start(), calls=%async_computation.3 | async-start | bytes 786432 | tf_op jit(solution)/shard_map/psum | solution.py:16
  49.3 363.5 %all-reduce.4.cloned.1.call-start = ((), (), s32[]{:S(2)}) async-start(), calls=%async_computation.2 | async-start | bytes 12582912 | tf_op jit(solution)/shard_map/psum | solution.py:18
  91.7 330.9 %reduce-scatter.2.cloned.1.call-start = ((), (), s32[]{:S(2)}) async-start(), calls=%async_computation.1 | async-start | bytes 9437184 | tf_op jit(solution)/shard_map/reduce_scatter | solution.py:17
Sparse Core Ops, SparseCore 0:
  49.5 138.9 all-reduce.5
  190.8 221.9 all-reduce.3
Sparse Core Ops, SparseCore 1:
  95.7 74.4 reduce-scatter.1
where the time goes:
time: 432 us
  waiting for transfers between devices  254 us (59%)
  matrix products  98.5 us (23%)
  other arithmetic  55.8 us (13%)
  between operations  17.5 us (4%)
  local copies, waits for them, and re-layouts  5.54 us (1%)
    psum x1, waiting for transfers between devices, body(): lax.psum(lax.dot_general(operator, left_test, (((0,), (0,)), ((), ())), p...  158 us
    psum x1, waiting for transfers between devices, body(): core_matrix = lax.psum(block_core, ('row', 'col'))  96.1 us
    dot_general x1, matrix products, body(): lax.dot_general(operator, left_test, (((0,), (0,)), ((), ())), preferred_...  42.3 us
    another operation x6, other arithmetic, body(): lower_factor = jnp.linalg.cholesky(gram_matrix)  34 us
    dot_general x1, matrix products, body(): jnp.dot(operator, right_test, preferred_element_type=jnp.float32)  28.9 us
    another operation x3, other arithmetic, body(): solve_map = jax.scipy.linalg.cho_solve((lower_factor, True), core_matrix.T)  19.7 us
    dot_general x1, matrix products, body(): lax.dot_general(left_test.astype(jnp.float32), block_left, (((0,), (0,)),...  10.9 us
    dot_general x1, matrix products, body(): jnp.dot(right_whole, solve_map.T, precision=lax.Precision.HIGHEST)  9.8 us
  transfers between devices with their start and end apart: 3, of which 2 were waited for; matrix products, arithmetic and copies ran while one was open for 27% of the time, Pallas kernels for 0%

commit v1 on v0

v1 whole, which is shorter than its diff:
```python
import functools

import jax
import jax.numpy as jnp
from jax import lax
from jax.experimental import pallas as pl
from jax.experimental.pallas import tpu as pltpu
from jax.sharding import PartitionSpec as P

HIGHEST = lax.Precision.HIGHEST
F32 = jnp.float32
MESH = pl.DeviceIdType.MESH


def split3(x):
    a = x.astype(jnp.bfloat16)
    r = x - a.astype(F32)
    b = r.astype(jnp.bfloat16)
    c = (r - b.astype(F32)).astype(jnp.bfloat16)
    return a, b, c


def dot_rows(a, b, precision=None):
    return lax.dot_general(
        a, b, (((0,), (0,)), ((), ())), precision=precision, preferred_element_type=F32
    )


def bit_orders(count):
    bits = list(range(count.bit_length() - 1))
    return [bits, bits[:1] + bits[1:][::-1]]


def kernel(nr, nc, right_ref, left_ref, test_ref, left_out, right_out, *scratch):
    levels = nc.bit_length() - 1
    recv_left = scratch[:levels]
    (ring, core_own, core_col, core_row, core_all, work, solve_map,
     left_send, left_recv, ring_send, ring_recv, one_send, one_recv, two_send, two_recv,
     three_send, three_recv, ag_send, ag_recv) = scratch[levels:]
    row, col = lax.axis_index("row"), lax.axis_index("col")
    barrier = pltpu.get_barrier_semaphore()
    for i in range(1, nc):
        pl.semaphore_signal(barrier, inc=1, device_id={"col": lax.rem(col + i, nc)}, device_id_type=MESH)
    for i in range(1, nr):
        pl.semaphore_signal(barrier, inc=1, device_id={"row": lax.rem(row + i, nr)}, device_id_type=MESH)
    pl.semaphore_wait(barrier, nr + nc - 2)

    pending = []

    def send(src, dst, ssem, rsem, to):
        copy = pltpu.make_async_remote_copy(
            src_ref=src, dst_ref=dst, send_sem=ssem, recv_sem=rsem, device_id=to, device_id_type=MESH
        )
        copy.start()
        pending.append(copy)
        return copy

    chunk = right_ref.shape[0] // nr
    half = chunk // 2
    width = left_ref.shape[2]
    near = (lax.rem(row + 1, nr), lax.rem(row + nr - 1, nr))

    def rows_of(back, way):
        owner = lax.rem(row - back + 2 * nr, nr) if way == 0 else lax.rem(row + back, nr)
        return pl.ds(pl.multiple_of(owner * chunk + way * half, half), half)

    def ring_start(s):
        return [
            send(
                right_ref.at[rows_of(1, way)] if s == 0 else ring.at[way, s - 1],
                ring.at[way, s],
                ring_send.at[way, s],
                ring_recv.at[way, s],
                {"row": near[way]},
            )
            for way in range(2)
        ]

    def ring_add(s, copies):
        for way in range(2):
            copies[way].wait_recv()
            ring[way, s] += right_ref[rows_of(s + 2, way), :]

    orders = bit_orders(nc)
    lanes = width // 2

    def bit_of(b):
        return lax.rem(lax.div(col, 1 << b), 2)

    def left_index(order, level, e, flip):
        rest = order[level + 1:]
        total = jnp.int32(0)
        for b in order[: level + 1]:
            value = bit_of(b)
            if flip and b == order[level]:
                value = 1 - value
            total = total + value * (1 << b)
        for place, b in enumerate(rest):
            total = total + ((e >> place) & 1) * (1 << b)
        return total

    def left_source(h, level, e, flip):
        order = orders[h]
        if level == 0:
            return left_ref.at[left_index(order, 0, e, flip), :, pl.ds(h * lanes, lanes)]
        mine = bit_of(order[level])
        mine = 1 - mine if flip else mine
        return recv_left[level - 1].at[h, mine + 2 * e]

    def left_base(level):
        return sum(nc >> (l + 1) for l in range(level))

    def left_start(level):
        out = []
        for e in range(nc >> (level + 1)):
            for h in range(2):
                b = orders[h][level]
                partner = col + (1 - 2 * bit_of(b)) * (1 << b)
                at = left_base(level) + e
                out.append((h, e, send(
                    left_source(h, level, e, True),
                    recv_left[level].at[h, e],
                    left_send.at[h, at],
                    left_recv.at[h, at],
                    {"col": partner},
                )))
        return out

    def left_add(level, copies):
        for h, e, copy in copies:
            copy.wait_recv()
            recv_left[level][h, e] += left_source(h, level, e, False)[...]

    ring_now = ring_start(0)
    left_now = left_start(0)

    depth = left_ref.shape[1]

    core_own[...] = jnp.zeros_like(core_own)

    def core_step(c, carry):
        test = test_ref[pl.ds(pl.multiple_of(c * depth, depth), depth), :]
        a, b, d = split3(left_ref[c])
        core_own[...] += dot_rows(test, a) + (dot_rows(test, b) + dot_rows(test, d))
        return carry

    lax.fori_loop(0, nc, core_step, 0)

    piece = core_own.shape[0] // nc

    def piece_of(owner):
        return pl.ds(pl.multiple_of(owner * piece, piece), piece)

    one = []
    for i in range(1, nc):
        to = lax.rem(col + i, nc)
        one.append(send(core_own.at[piece_of(to)], core_col.at[i], one_send.at[i], one_recv.at[i], {"col": to}))
    for copy in one:
        copy.wait_recv()
    total = core_own[piece_of(col), :]
    for i in range(1, nc):
        total = total + core_col[i]
    core_row[0] = total
    two = []
    for i in range(1, nr):
        to = lax.rem(row + i, nr)
        two.append(send(core_row.at[0], core_row.at[i], two_send.at[i], two_recv.at[i], {"row": to}))
    left_add(0, left_now)
    ring_add(0, ring_now)
    if nr > 2:
        ring_now = ring_start(1)
    for copy in two:
        copy.wait_recv()
    for i in range(1, nr):
        total = total + core_row[i]
    core_all[piece_of(col), :] = total
    three = []
    for i in range(1, nc):
        to = lax.rem(col + i, nc)
        three.append(send(
            core_all.at[piece_of(col)], core_all.at[piece_of(col)], three_send.at[i], three_recv.at[i], {"col": to}
        ))
    left_now = left_start(1) if levels > 1 else None
    for copy in three:
        copy.wait_recv()

    core = core_all[...]
    gram = dot_rows(core, core, HIGHEST)
    ids = lax.broadcasted_iota(jnp.int32, (width, width), 0)
    cols = lax.broadcasted_iota(jnp.int32, (width, width), 1)
    shift = 0.001 * jnp.sum(jnp.where(ids == cols, gram, 0.0)) / width
    work[...] = gram + jnp.where(ids == cols, shift, 0.0)
    lane = lax.broadcasted_iota(jnp.int32, (1, width), 1)

    def step(k, carry):
        held = work[...]
        line = work[pl.ds(k, 1), :]
        at_k = cols == k
        column = jnp.sum(jnp.where(at_k, held, 0.0), axis=1, keepdims=True)
        pivot = 1.0 / jnp.sum(jnp.where(lane == k, line, 0.0), axis=1, keepdims=True)
        scaled = jnp.where(lane == k, pivot, line * pivot)
        work[...] = jnp.where(at_k, 0.0, held) - column * scaled
        work[pl.ds(k, 1), :] = scaled
        return carry

    jobs = []
    for s in range(1, nr - 1):
        jobs.append(("ring", s))
        if s < levels:
            jobs.append(("left", s))
    for level in range(nr - 1, levels):
        jobs.append(("left", level))
    if nr <= 2:
        jobs = [("left", level) for level in range(1, levels)]
    cut = len(jobs) + 1
    edges = [width * j // cut for j in range(cut + 1)]
    for j in range(cut):
        lax.fori_loop(edges[j], edges[j + 1], step, 0)
        if j < len(jobs):
            kind, s = jobs[j]
            if kind == "ring":
                ring_add(s, ring_now)
                if s < nr - 2:
                    ring_now = ring_start(s + 1)
            else:
                left_add(s, left_now)
                if s < levels - 1:
                    left_now = left_start(s + 1)
    solve_map[...] = jnp.dot(core, work[...], precision=HIGHEST, preferred_element_type=F32)

    def ag_start(s):
        out = []
        for way in range(2):
            part = right_out.at[rows_of(s, way)]
            out.append(send(part, part, ag_send.at[way, s], ag_recv.at[way, s], {"row": near[way]}))
        return out

    for way in range(2):
        right_out[rows_of(0, way), :] = jnp.dot(
            ring[way, nr - 2], solve_map[...], precision=HIGHEST, preferred_element_type=F32
        ).astype(jnp.bfloat16)
    ag_now = ag_start(0)
    for h in range(2):
        left_out[:, h * lanes:(h + 1) * lanes] = recv_left[levels - 1][h, 0].astype(jnp.bfloat16)
    for s in range(1, nr):
        for copy in ag_now:
            copy.wait_recv()
        if s < nr - 1:
            ag_now = ag_start(s)
    for copy in pending:
        copy.wait_send()


def exchange(nr, nc, right_block, left_block, left_test):
    rows, wide = right_block.shape
    depth, width = left_block.shape
    depth = depth // nc
    levels = nc.bit_length() - 1
    half = rows // nr // 2
    vmem = pl.BlockSpec(memory_space=pltpu.VMEM)
    dma = pltpu.SemaphoreType.DMA
    scratch = [pltpu.VMEM((2, nc >> (l + 1), depth, width // 2), F32) for l in range(levels)]
    scratch += [
        pltpu.VMEM((2, nr - 1, half, wide), F32),
        pltpu.VMEM((wide, width), F32),
        pltpu.VMEM((nc, wide // nc, width), F32),
        pltpu.VMEM((nr, wide // nc, width), F32),
        pltpu.VMEM((wide, width), F32),
        pltpu.VMEM((width, width), F32),
        pltpu.VMEM((wide, width), F32),
        dma((2, nc - 1)), dma((2, nc - 1)),
        dma((2, nr - 1)), dma((2, nr - 1)),
        dma((nc,)), dma((nc,)),
        dma((nr,)), dma((nr,)),
        dma((nc,)), dma((nc,)),
        dma((2, nr - 1)), dma((2, nr - 1)),
    ]
    return pl.pallas_call(
        functools.partial(kernel, nr, nc),
        out_shape=(
            jax.ShapeDtypeStruct((depth, width), jnp.bfloat16),
            jax.ShapeDtypeStruct((rows, width), jnp.bfloat16),
        ),
        in_specs=[vmem] * 3,
        out_specs=(vmem, vmem),
        scratch_shapes=scratch,
        compiler_params=pltpu.CompilerParams(
            collective_id=0, has_side_effects=True, vmem_limit_bytes=60 * 1024 * 1024
        ),
    )(right_block, left_block.reshape(nc, depth, width), left_test)


def body(nr, nc, operator, right_test, left_test):
    right_block = lax.dot_general(
        operator, left_test, (((0,), (0,)), ((), ())), preferred_element_type=F32
    )
    block_left = jnp.dot(operator, right_test, preferred_element_type=F32)
    return exchange(nr, nc, right_block, block_left, left_test)


def solution(mesh):
    placed = (P("row", "col"), P("col", None), P("row", None))
    return jax.shard_map(
        functools.partial(body, mesh.shape["row"], mesh.shape["col"]),
        mesh=mesh,
        in_specs=placed,
        out_specs=(P(("row", "col"), None), P("col", None)),
        check_vma=False,
    )
```

time: 432 us -> 252 us (0.58)
  waiting for transfers between devices: 254 us -> 0 us
  Pallas kernels: 0 us -> 174 us
  other arithmetic: 55.8 us -> 0 us
  matrix products: 98.5 us -> 71.3 us
  between operations: 17.5 us -> 0.65 us
    psum x2 -> x0, waiting for transfers between devices: 254 us -> none  [the longest x1 158 us: body(): lax.psum(lax.dot_general(operator, left_test, (((0,), (0,)), ((), ())), p...]
    pallas_call x0 -> x1, Pallas kernels: none -> 174 us  [exchange(): pl.pallas_call(functools.partial(kernel, nr, nc), out_shape=(jax.ShapeDty...]
    another operation x9 -> x0, other arithmetic: 53.7 us -> none  [the longest x6 34 us: body(): lower_factor = jnp.linalg.cholesky(gram_matrix)]
    dot_general x4 -> x1, matrix products: 51.9 us -> 28.9 us  [body(): block_left = jnp.dot(operator, right_test, preferred_element_type=F32)]
    another operation x8 -> x0, matrix products: 4.36 us -> none  [the longest x6 3.89 us: body(): solve_map = jax.scipy.linalg.cho_solve((lower_factor, True), core_matrix.T)]
  transfers between devices with their start and end apart: 3 -> 0, of which waited for: 2 -> 0; matrix products, arithmetic and copies ran while one was open for 27% -> 0% of each run, Pallas kernels for 0% -> 0%
where the time goes in v1:
time: 252 us; the launch traced here: 251 us
  Pallas kernels  174 us (69%)
  matrix products  71.3 us (28%)
  local copies, waits for them, and re-layouts  4.92 us (2%)
    pallas_call x1, Pallas kernels, exchange(): pl.pallas_call(functools.partial(kernel, nr, nc), out_shape=(jax.ShapeDty...  174 us
    dot_general x1, matrix products, body(): lax.dot_general(operator, left_test, (((0,), (0,)), ((), ())), preferred_...  42.4 us
    dot_general x1, matrix products, body(): block_left = jnp.dot(operator, right_test, preferred_element_type=F32)  28.9 us

profile of v1, /device:TPU:0, one launch (start us, length us, event | category | flops | bytes accessed | tf_op | source)
XLA Modules:
  0.0 251.3 jit_solution(16705692103393462573)
XLA Ops:
  0.6 0.0 copy-start
  0.6 42.4 %fusion.right_ref = f32[4096,384]{1,0:T(8,128)} fusion(bf16[8192,4096]{1,0:T(8,128)(2,1)} %param.3, bf16[8192,384]{1,0:T(8,128)(2,1)} %test_ref.1), kind=kOutput, calls=%fused_computation | convolution fusion | flops 25769803776 | bytes 79691776 | tf_op jit(solution)/shard_map/dot_general | solution.py:294
  43.1 0.0 copy-done
  43.1 28.9 %fusion.1 = f32[8192,256]{1,0:T(8,128)} fusion(bf16[8192,4096]{1,0:T(8,128)(2,1)} %param.3, bf16[4096,256]{1,0:T(8,128)(2,1)S(1)} %copy-done), kind=kOutput, calls=%fused_computation.1 | convolution fusion | flops 17179869184 | bytes 77594624 | tf_op jit(solution)/shard_map/dot_general | solution.py:297
  71.9 174.4 %shard_map.50 = (bf16[1024,256]{1,0:T(8,128)(2,1)}, bf16[4096,256]{1,0:T(8,128)(2,1)}) custom-call(f32[4096,384]{1,0:T(8,128)} %fusion.right_ref, f32[8,1024,256]{2,1,0:T(8,128)} %bitcast.5, bf16[8192,384]{1,0:T(8,128)(2,1)} %test_ref.1), custom_call_target="tpu_custom_call" | custom-call | tf_op jit(solution)/shard_map/pallas_call | solution.py:278
  246.4 1.9 copy.7
  248.2 3.0 %copy.8 = bf16[4096,256]{1,0:T(8,128)(2,1)} copy(bf16[4096,256]{1,0:T(8,128)(2,1)} %get-tuple-element.5) | data formatting | bytes 4194304
Async XLA Ops:
  0.6 42.5 %copy-start = (bf16[4096,256]{1,0:T(8,128)(2,1)S(1)}, bf16[4096,256]{1,0:T(8,128)(2,1)}, u32[]{:S(2)}) copy-start(bf16[4096,256]{1,0:T(8,128)(2,1)} %param.4) | copy-start | bytes 6291460
